TPU v7x, 32 devices: a whole 2x2x4 slice. The times are simulated.
32 devices in a mesh: seq: 8 (over z, y), batch: 4 (over x, core).
Axes of the slice: x: 2, y: 2, z: 4, core: 2. Of those that a mesh axis runs over, the one named last changes fastest.
Arguments:
- queries: bfloat16 [4, 4096, 16, 128], P('batch', 'seq'), may hold values from -5 to 5
- keys: bfloat16 [4, 4096, 16, 128], P('batch', 'seq'), may hold values from -5 to 5
- values: bfloat16 [4, 4096, 16, 128], P('batch', 'seq'), may hold values from -5 to 5
- keep_count: int32 [4, 16, 32], P('batch'), may hold values from 0 to 128
- query_map: bfloat16 [16, 128, 8], replicated, may hold values from -0.5 to 0.5
- key_map: bfloat16 [16, 128, 8], replicated, may hold values from -0.5 to 0.5
- cotangent: bfloat16 [4, 4096, 16, 128], P('batch', 'seq'), may hold values from -5 to 5
Outputs:
- attended: bfloat16 [4, 4096, 16, 128], P('batch', 'seq')
- grad_query_map: float32 [16, 128, 8], replicated
- grad_key_map: float32 [16, 128, 8], replicated
All inputs are finite; a program needn't handle non-finite values.
Results may differ from a plain program's by a relative error of at most 0.0035.
Values may be sent and summed in bfloat16 or wider, within the bound.
A program may use at most 128 MiB of HBM per device.

v0:
```python
import math
import jax
import jax.numpy as jnp
from jax import lax
from jax.sharding import PartitionSpec as P

TILE = 128
WINDOW = 256
HIGHEST = lax.Precision.HIGHEST
feature_shift = 1.5


def passed_along(value, axis, steps):
    count = lax.axis_size(axis)
    first, last = (max(0, -steps), min(count, count - steps))
    return lax.ppermute(value, axis, [(source, source + steps) for source in range(first, last)])


def prefix(shard, axis, combine, identity, reverse):
    peers, position = (lax.axis_size(axis), lax.axis_index(axis))
    everything = jax.tree.map(lambda part: lax.all_gather(part, axis), shard)
    start = jax.tree.map(
        lambda part, zero: jnp.broadcast_to(jnp.asarray(zero, part.dtype), part.shape),
        shard,
        identity,
    )

    def step(k, before):
        at = peers - 1 - k if reverse else k
        reached = at > position if reverse else at < position
        new = combine(before, jax.tree.map(lambda part: part[at], everything))
        return jax.tree.map(lambda a, b: jnp.where(reached, a, b), new, before)

    return lax.fori_loop(0, peers, step, start)


def add_pair(earlier, later):
    return (earlier[0] + later[0], earlier[1] + later[1])


def windowed(tiled, first, count, span):
    pieces = [
        lax.slice_in_dim(tiled, first + offset, first + offset + count, axis=0)
        for offset in range(span)
    ]
    return jnp.concatenate(pieces, 1)


def body(queries, keys, values, keep_count, query_map, key_map, cotangent):
    q_rows = queries[0]
    k_rows = keys[0]
    v_rows = values[0]
    cot_rows = cotangent[0].astype(jnp.float32)
    tokens, heads, width = q_rows.shape
    rank = query_map.shape[2]
    tiles_dev = tokens // TILE
    span = WINDOW // TILE
    scale = 1.0 / math.sqrt(width)
    index = lax.axis_index("seq")
    halo_rows = WINDOW - TILE
    prev_keys, prev_values = passed_along(
        (k_rows[tokens - halo_rows :], v_rows[tokens - halo_rows :]), "seq", 1
    )
    halo_tiles = halo_rows // TILE
    ext_tiles = halo_tiles + tiles_dev
    ext_rows = halo_rows + tokens
    ext_keys = jnp.concatenate([prev_keys, k_rows], 0)
    ext_values = jnp.concatenate([prev_values, v_rows], 0)
    counts = keep_count[0]
    padded_counts = jnp.concatenate([jnp.zeros((heads, tiles_dev), jnp.int32), counts], 1)
    count_start = index * tiles_dev + tiles_dev - halo_tiles
    ext_counts = lax.dynamic_slice_in_dim(padded_counts, count_start, ext_tiles, 1)
    local = jnp.arange(ext_rows, dtype=jnp.int32)
    key_pos = index * tokens - halo_rows + local
    valid = key_pos >= 0
    within = local % TILE
    kept = within[None, :] < jnp.repeat(ext_counts, TILE, axis=1)
    evicted = valid[None, :] & jnp.logical_not(kept)
    pre_q = (
        jnp.einsum("thd,hdr->thr", q_rows, query_map, preferred_element_type=jnp.float32)
        - feature_shift
    )
    pre_k = (
        jnp.einsum("thd,hdr->thr", ext_keys, key_map, preferred_element_type=jnp.float32)
        - feature_shift
    )
    feat_q = jax.nn.softplus(pre_q)
    feat_k = jax.nn.softplus(pre_k)
    valid_f = valid.astype(jnp.float32)[:, None, None]
    evict_f = evicted.T.astype(jnp.float32)[:, :, None]
    v_tiles = ext_values.astype(jnp.float32).reshape(ext_tiles, TILE, heads, width)

    def tile_state(feat):
        tiled = feat.reshape(ext_tiles, TILE, heads, rank)
        return (jnp.einsum("nthr,nthd->nhrd", tiled, v_tiles, precision=HIGHEST), jnp.sum(tiled, 1))

    all_state, all_norm = tile_state(feat_k * valid_f)
    ev_state, ev_norm = tile_state(feat_k * evict_f)
    q_tile = jnp.arange(tiles_dev, dtype=jnp.int32)[:, None] + halo_tiles
    k_tile = jnp.arange(ext_tiles, dtype=jnp.int32)[None, :]
    in_halo = (k_tile < halo_tiles).astype(jnp.float32)
    far_mix = (k_tile < q_tile - span + 1).astype(jnp.float32)
    near_mix = ((k_tile >= q_tile - span + 1) & (k_tile < q_tile)).astype(jnp.float32)
    far_coef = far_mix * (1.0 - in_halo) - near_mix * in_halo
    carried_state = jnp.sum(all_state[halo_tiles:], 0)
    carried_norm = jnp.sum(all_norm[halo_tiles:], 0)
    far_state, far_norm = prefix(
        (carried_state, carried_norm),
        "seq",
        add_pair,
        (jnp.zeros_like(carried_state), jnp.zeros_like(carried_norm)),
        False,
    )
    state = (
        far_state[None]
        + jnp.einsum("jn,nhrd->jhrd", far_coef, all_state, precision=HIGHEST)
        + jnp.einsum("jn,nhrd->jhrd", near_mix, ev_state, precision=HIGHEST)
    )
    norm = (
        far_norm[None]
        + jnp.einsum("jn,nhr->jhr", far_coef, all_norm, precision=HIGHEST)
        + jnp.einsum("jn,nhr->jhr", near_mix, ev_norm, precision=HIGHEST)
    )
    first_tile = halo_tiles - span + 1
    key_window = windowed(
        ext_keys.reshape(ext_tiles, TILE, heads, width), first_tile, tiles_dev, span
    )
    value_window = windowed(
        ext_values.reshape(ext_tiles, TILE, heads, width), first_tile, tiles_dev, span
    )
    allowed = (kept & valid[None, :]).T.reshape(ext_tiles, TILE, heads)
    allowed_window = windowed(allowed, first_tile, tiles_dev, span).transpose(0, 2, 1)
    slot = jnp.arange(span * TILE, dtype=jnp.int32)
    own_slot = slot >= (span - 1) * TILE
    causal = slot[None, :] - (span - 1) * TILE <= jnp.arange(TILE, dtype=jnp.int32)[:, None]
    live_pairs = jnp.where(
        own_slot[None, None, None, :], causal[None, None], allowed_window[:, :, None, :]
    )
    q_tiles = q_rows.reshape(tiles_dev, TILE, heads, width)
    scores = (
        jnp.einsum("nqhd,nkhd->nhqk", q_tiles, key_window, preferred_element_type=jnp.float32)
        * scale
    )
    row_max = jnp.max(jnp.where(live_pairs, scores, -jnp.inf), -1)
    weights = jnp.where(live_pairs, jnp.exp(scores - row_max[..., None]), 0.0)
    denom = jnp.sum(weights, -1).transpose(0, 2, 1).reshape(tokens, heads)
    numer = jnp.einsum(
        "nhqk,nkhd->nqhd",
        weights.astype(jnp.bfloat16),
        value_window,
        preferred_element_type=jnp.float32,
    ).reshape(tokens, heads, width)
    decay = jnp.exp(-row_max.transpose(0, 2, 1).reshape(tokens, heads))
    feat_qt = feat_q.reshape(tiles_dev, TILE, heads, rank)
    kernel_num = jnp.einsum("nthr,nhrd->nthd", feat_qt, state, precision=HIGHEST).reshape(
        tokens, heads, width
    )
    kernel_den = jnp.einsum("nthr,nhr->nth", feat_qt, norm, precision=HIGHEST).reshape(
        tokens, heads
    )
    total = denom + decay * kernel_den
    out = (numer + decay[..., None] * kernel_num) / total[..., None]
    delta = cot_rows / total[..., None]
    ratio_grad = -jnp.sum(delta * out, -1)
    grad_num = (decay[..., None] * delta).reshape(tiles_dev, TILE, heads, width)
    grad_den = (decay * ratio_grad).reshape(tiles_dev, TILE, heads)
    grad_fq = (
        jnp.einsum("nthd,nhrd->nthr", grad_num, state, precision=HIGHEST)
        + grad_den[..., None] * norm[:, None]
    )
    d_state = jnp.einsum("nthr,nthd->nhrd", feat_qt, grad_num, precision=HIGHEST)
    d_norm = jnp.einsum("nthr,nth->nhr", feat_qt, grad_den, precision=HIGHEST)
    own_state = jnp.sum(d_state, 0)
    own_norm = jnp.sum(d_norm, 0)
    after_state, after_norm = prefix(
        (own_state, own_norm),
        "seq",
        add_pair,
        (jnp.zeros_like(own_state), jnp.zeros_like(own_norm)),
        True,
    )
    own_tiles = (jnp.arange(ext_tiles, dtype=jnp.int32) >= halo_tiles).astype(jnp.float32)
    d_all = (
        jnp.einsum("jn,jhrd->nhrd", far_coef, d_state, precision=HIGHEST)
        + own_tiles[:, None, None, None] * after_state[None]
    )
    d_alln = (
        jnp.einsum("jn,jhr->nhr", far_coef, d_norm, precision=HIGHEST)
        + own_tiles[:, None, None] * after_norm[None]
    )
    d_ev = jnp.einsum("jn,jhrd->nhrd", near_mix, d_state, precision=HIGHEST)
    d_evn = jnp.einsum("jn,jhr->nhr", near_mix, d_norm, precision=HIGHEST)
    grad_all = jnp.einsum("nhrd,nthd->nthr", d_all, v_tiles, precision=HIGHEST) + d_alln[:, None]
    grad_ev = jnp.einsum("nhrd,nthd->nthr", d_ev, v_tiles, precision=HIGHEST) + d_evn[:, None]
    grad_fk = valid_f * grad_all.reshape(ext_rows, heads, rank) + evict_f * grad_ev.reshape(
        ext_rows, heads, rank
    )
    grad_pre_k = grad_fk * jax.nn.sigmoid(pre_k)
    grad_pre_q = grad_fq.reshape(tokens, heads, rank) * jax.nn.sigmoid(pre_q)
    grad_q = jnp.einsum("thd,thr->hdr", q_rows.astype(jnp.float32), grad_pre_q, precision=HIGHEST)
    grad_k = jnp.einsum("thd,thr->hdr", ext_keys.astype(jnp.float32), grad_pre_k, precision=HIGHEST)
    grad_q, grad_k = lax.psum((grad_q, grad_k), ("seq", "batch"))
    return (out.astype(jnp.bfloat16)[None], grad_q, grad_k)


def solution(mesh):
    placed = (
        P("batch", "seq", None, None),
        P("batch", "seq", None, None),
        P("batch", "seq", None, None),
        P("batch", None, None),
        P(),
        P(),
        P("batch", "seq", None, None),
    )
    return jax.shard_map(
        body,
        mesh=mesh,
        in_specs=placed,
        out_specs=(P("batch", "seq", None, None), P(), P()),
        check_vma=False,
    )
```

profile of v0, /device:TPU:0, one launch (start us, length us, event | category | flops | bytes accessed | tf_op | source)
XLA Modules:
  0.0 420.2 jit_solution(9056168187303462686)
XLA Ops:
  7.2 2.3 copy.332
  11.7 5.7 %collective-permute-start.1 = (bf16[128,16,128]{2,0,1:T(8,128)(2,1)}, bf16[128,16,128]{2,0,1:T(8,128)(2,1)}, u32[]{:S(2)}, u32[]{:S(2)}) collective-permute-start(bf16[128,16,128]{2,0,1:T(8,128)(2,1)} %slice_bitcast_fusion), channel_id=1, source_target_pairs={{0,4},{4,8},{8,12},{12,16},{16,20},{20,24},{24,28},{1,5},{5,9},{9,... | collective-permute-start | bytes 1572872 | tf_op jit(solution)/shard_map/ppermute | solution.py:16
  17.4 1.9 slice_bitcast_fusion.1
  19.3 2.7 collective-permute-start
  26.0 3.5 copy.177
  29.5 1.9 copy.171
  31.4 2.4 convert.3
  35.3 2.0 fusion.65
  43.1 2.1 fusion.44
  45.3 35.2 %all-gather = f32[128,8,128]{2,1,0:T(8,128)} all-gather(f32[16,8,128]{2,1,0:T(8,128)S(1)} %slice_reduce_fusion), channel_id=2, replica_groups=mesh['seq'=8,'batch'=4] {'seq'}, dimensions={0}, use_global_device_ids=true | all-gather | bytes 589824 | tf_op jit(solution)/shard_map/all_gather | solution.py:21
  80.6 30.6 %all-gather.4 = f32[8,16,8]{1,2,0:T(8,128)S(1)} all-gather(f32[1,16,8]{1,2,0:T(8,128)S(1)} %bitcast.246), channel_id=3, replica_groups=mesh['seq'=8,'batch'=4] {'seq'}, dimensions={0}, use_global_device_ids=true | all-gather | bytes 4608 | tf_op jit(solution)/shard_map/all_gather | solution.py:21
  111.2 7.7 %while.34 = (s32[]{:T(128)}, f32[16,8,128]{2,1,0:T(8,128)S(1)}, f32[16,8]{0,1:T(8,128)S(1)}, s32[]{:T(128)}, f32[8,16,8,128]{3,2,1,0:T(8,128)}, /*index=5*/f32[8,16,8]{1,2,0:T(8,128)S(1)}, s32[]{:T(128)}, s32[]{:T(128)}) while((s32[]{:T(128)}, f32[16,8,128]{2,1,0:T(8,128)S(1)}, f32[16,8]{0,1:T(8,128)S(1)}, s32[]{:T(128)}, ...), condition=%wide.region_5.6_spmd.clone, body=%wide.region_4.5_spmd.clone.sunk | while | flops 49540 | bytes 198259 | solution.py:34
  118.9 3.9 fusion.42
  124.9 6.7 %convolution_bitcast_fusion = f32[4,128,16,128]{3,1,2,0:T(8,128)S(1)} fusion(f32[4,16,8,128]{3,0,2,1:T(4,128)S(1)} %fusion.66, f32[512,16,8]{0,2,1:T(8,128)S(1)} %copy-done.13), kind=kOutput, calls=%fused_computation.42 | convolution fusion | flops 101056512 | bytes 4718592 | tf_op jit(solution)/shard_map/nthr,nhrd->nthd/dot_general | solution.py:155
  131.6 4.5 %copy.193 = f32[4,128,16,128]{3,2,1,0:T(8,128)} copy(f32[4,128,16,128]{3,1,2,0:T(8,128)S(1)} %convolution_bitcast_fusion) | data formatting | bytes 8388608 | tf_op jit(solution)/shard_map/nthr,nhrd->nthd/transpose | solution.py:155
  139.9 2.9 fusion
  143.5 4.1 fusion.2
  152.3 6.3 %fusion.27 = f32[4,128,16,128]{3,1,2,0:T(8,128)S(1)} fusion(f32[4,16,256,128]{3,2,1,0:T(8,128)S(1)} %copy-done.10, f32[4,16,128]{2,1,0:T(8,128)S(1)} %get-tuple-element.356, pred[4,16,256]{2,1,0:T(8,128)(4,1)S(1)} %copy-done.26, pred[128,256]{0,1:T(8,128)(4,1)S(1)} %copy-done.21, pred[256]{0:T(512)(128)(4,1)S(1)} %copy-done.42, ...), kind=kOutput, calls=%fused_computation.41 | convolution fusion | flops 555745280 | bytes 16859392 | tf_op jit(solution)/shard_map/nhqk,nkhd->nqhd/dot_general | solution.py:147
  158.6 4.4 %copy.180 = f32[4,128,16,128]{3,2,1,0:T(8,128)} copy(f32[4,128,16,128]{3,1,2,0:T(8,128)S(1)} %fusion.27) | data formatting | bytes 8388608 | tf_op jit(solution)/shard_map/nhqk,nkhd->nqhd/transpose | solution.py:147
  163.1 6.9 %fusion.14 = f32[512,16,128]{2,1,0:T(8,128)S(1)} fusion(f32[4,128,16,128]{3,2,1,0:T(8,128)} %copy.193, f32[4,128,16,128]{3,2,1,0:T(8,128)} %copy.180, f32[512,16]{1,0:T(8,128)S(1)} %copy.182, f32[512,16]{1,0:T(8,128)S(1)} %copy.198), kind=kLoop, calls=%fused_computation.21 | loop fusion | flops 3145728 | bytes 12648448 | tf_op jit(solution)/shard_map/div | solution.py:162
  170.0 14.1 %fusion.23 = f32[512,16]{1,0:T(8,128)S(1)} fusion(f32[512,16,128]{2,1,0:T(8,128)S(1)} %fusion.14, f32[512,16]{1,0:T(8,128)S(1)} %copy.198, bf16[1,512,16,128]{3,2,1,0:T(8,128)(2,1)S(1)} %copy-done.8), kind=kLoop, calls=%fused_computation.33 | loop fusion | flops 4186112 | bytes 6356992 | tf_op jit(solution)/shard_map/reduce_sum | solution.py:164
  186.7 7.5 %fusion.174 = (f32[16,8,128]{2,1,0:T(8,128)S(1)}, f32[4,16,8,128]{3,2,1,0:T(8,128)}) fusion(f32[4,128,16,128]{3,2,1,0:T(8,128)} %convert.3, f32[4,128,16]{1,2,0:T(8,128)S(1)} %get-tuple-element.351, f32[4,128,16]{1,2,0:T(8,128)S(1)} %copy-done.28, f32[512,16,8]{0,2,1:T(8,128)S(1)} %copy-done.14), kind=kOutput, calls=%fused_computation.200 | convolution fusion | flops 103202816 | bytes 4849664 | tf_op jit(solution)/shard_map/nthr,nthd->nhrd/dot_general | solution.py:171
  194.2 31.2 %all-gather.2 = f32[128,8,128]{2,1,0:T(8,128)S(1)} all-gather(f32[16,8,128]{2,1,0:T(8,128)S(1)} %get-tuple-element.358), channel_id=4, replica_groups=mesh['seq'=8,'batch'=4] {'seq'}, dimensions={0}, use_global_device_ids=true | all-gather | bytes 589824 | tf_op jit(solution)/shard_map/all_gather | solution.py:21
  225.4 30.6 %all-gather.5 = f32[8,16,8]{1,2,0:T(8,128)S(1)} all-gather(f32[1,16,8]{1,2,0:T(8,128)S(1)} %bitcast.245), channel_id=5, replica_groups=mesh['seq'=8,'batch'=4] {'seq'}, dimensions={0}, use_global_device_ids=true | all-gather | bytes 4608 | tf_op jit(solution)/shard_map/all_gather | solution.py:21
  258.7 2.6 convolution_add_fusion
  262.2 9.5 %fusion.76 = f32[4,128,16,8]{1,3,2,0:T(8,128)S(1)} fusion(f32[4,128,16,128]{3,2,1,0:T(8,128)} %convert.3, f32[4,128,16]{1,2,0:T(8,128)} %copy-done.31, f32[4,128,16]{1,2,0:T(8,128)} %get-tuple-element.352, f32[4,16,8,128]{3,0,2,1:T(4,128)} %copy-done.15, f32[4,16,8]{2,1,0:T(8,128)} %copy.207, f32[4,128,16]{1,2,0:T(8,128)} %copy-done.30), kind=kOutput, calls=%fused_computation.74 | convolution fusion | flops 102891520 | bytes 4818944 | tf_op jit(solution)/shard_map/nthd,nhrd->nthr/dot_general | solution.py:168
  271.7 2.0 fusion.79
  273.7 4.1 fusion.51
  277.9 4.1 fusion.57
  282.1 3.1 fusion.47
  285.1 7.2 %fusion.18 = bf16[1,512,16,128]{3,2,1,0:T(8,128)(2,1)} fusion(f32[512,16]{1,0:T(8,128)S(1)} %copy.198, f32[512,16]{1,0:T(8,128)S(1)} %copy.182, f32[1,512,16,128]{3,2,1,0:T(8,128)} %bitcast.221, f32[1,512,16,128]{3,2,1,0:T(8,128)} %bitcast.222), kind=kLoop, calls=%fused_computation.27 | loop fusion | flops 4194304 | bytes 10551296 | tf_op jit(solution)/shard_map/convert_element_type | solution.py:203
  292.4 117.7 %all-reduce.4.cloned.1.call-done = (f32[16,128,8]{1,2,0:T(8,128)}, f32[16,128,8]{1,2,0:T(8,128)}) async-done(((f32[16,128,8]{1,2,0:T(8,128)}, f32[16,128,8]{1,2,0:T(8,128)}), (f32[16,128,8]{1,2,0:T(8,128)}, f32[16,128,8]{1,2,0:T(8,128)})) %all-reduce.4.cloned.1.call-update) | async-done | bytes 131088 | tf_op jit(solution)/shard_map/psum | solution.py:202
  (186 shorter events, 40.9 us)
Async XLA Ops:
  7.2 26.6 %copy-start = (bf16[1,512,16,128]{3,2,1,0:T(8,128)(2,1)S(1)}, bf16[1,512,16,128]{3,2,1,0:T(8,128)(2,1)}, u32[]{:S(2)}) copy-start(bf16[1,512,16,128]{3,2,1,0:T(8,128)(2,1)} %param.11) | copy-start | bytes 6291460
  7.2 16.6 %copy-start.37 = (s32[1,16,32]{2,1,0:T(8,128)S(1)}, s32[1,16,32]{2,1,0:T(8,128)}, u32[]{:S(2)}) copy-start(s32[1,16,32]{2,1,0:T(8,128)} %param.14) | copy-start | bytes 6148
  7.2 402.9 %all-reduce.4.cloned.1.call-start = ((), (), s32[]{:S(2)}) async-start(), calls=%async_computation | async-start | bytes 262144 | tf_op jit(solution)/shard_map/psum | solution.py:202
  11.7 23.6 %collective-permute-start.1 = (bf16[128,16,128]{2,0,1:T(8,128)(2,1)}, bf16[128,16,128]{2,0,1:T(8,128)(2,1)}, u32[]{:S(2)}, u32[]{:S(2)}) collective-permute-start(bf16[128,16,128]{2,0,1:T(8,128)(2,1)} %slice_bitcast_fusion), channel_id=1, source_target_pairs={{0,4},{4,8},{8,12},{12,16},{16,20},{20,24},{24,28},{1,5},{5,9},{9,... | collective-permute-start | bytes 1572872 | tf_op jit(solution)/shard_map/ppermute | solution.py:16
  19.3 20.4 %collective-permute-start = (bf16[128,16,128]{2,1,0:T(8,128)(2,1)}, bf16[128,16,128]{2,1,0:T(8,128)(2,1)S(1)}, u32[]{:S(2)}, u32[]{:S(2)}) collective-permute-start(bf16[128,16,128]{2,1,0:T(8,128)(2,1)} %slice_bitcast_fusion.1), channel_id=1, source_target_pairs={{0,4},{4,8},{8,12},{12,16},{16,20},{20,24},{24,28},{1,5},{5,9},{9,... | collective-permute-start | bytes 1572872 | tf_op jit(solution)/shard_map/ppermute | solution.py:16
  22.0 15.3 %copy-start.32 = (f32[640]{0:T(1024)}, f32[640]{0:T(1024)S(1)}, u32[]{:S(2)}) copy-start(f32[640]{0:T(1024)S(1)} %fusion.149) | copy-start | bytes 7684
  22.0 114.2 %copy-start.34 = (s32[4]{0:T(128)}, s32[4]{0:T(128)S(1)}, u32[]{:S(2)}) copy-start(s32[4]{0:T(128)S(1)} %iota_add_fusion.1) | copy-start | bytes 52
  25.4 4.1 copy-start.3
  31.4 4.0 copy-start.44
  111.2 12.2 %copy-start.38 = (f32[5]{0:T(128)S(1)}, f32[5]{0:T(128)}, u32[]{:S(2)}) copy-start(f32[5]{0:T(128)} %broadcast_subtract_fusion) | copy-start | bytes 64
  111.2 12.2 %copy-start.40 = (f32[5]{0:T(128)S(1)}, f32[5]{0:T(128)}, u32[]{:S(2)}) copy-start(f32[5]{0:T(128)} %compare_convert_fusion.1) | copy-start | bytes 64
  118.9 6.0 %copy-start.13 = (f32[512,16,8]{0,2,1:T(8,128)S(1)}, f32[512,16,8]{0,2,1:T(8,128)}, u32[]{:S(2)}) copy-start(f32[512,16,8]{0,2,1:T(8,128)} %fusion.73) | copy-start | bytes 786436
  131.6 4.7 %copy-start.29 = (f32[5,16,8]{1,0,2:T(8,128)S(1)}, f32[5,16,8]{1,0,2:T(8,128)}, u32[]{:S(2)}) copy-start(f32[5,16,8]{1,0,2:T(8,128)} %copy.195) | copy-start | bytes 7684
  131.6 5.8 %copy-start.14 = (f32[512,16,8]{0,2,1:T(8,128)S(1)}, f32[512,16,8]{0,2,1:T(8,128)}, u32[]{:S(2)}) copy-start(f32[512,16,8]{0,2,1:T(8,128)} %fusion.73) | copy-start | bytes 786436
  138.2 10.1 %copy-start.23 = (f32[4,16,1,128]{3,2,1,0:T(1,128)}, f32[4,16,1,128]{3,2,1,0:T(1,128)S(1)}, u32[]{:S(2)}) copy-start(f32[4,16,1,128]{3,2,1,0:T(1,128)S(1)} %fusion.112) | copy-start | bytes 98308
  142.8 4.8 %copy-start.9 = (f32[4,16,256,128]{3,2,1,0:T(8,128)}, f32[4,16,256,128]{3,2,1,0:T(8,128)S(1)}, u32[]{:S(2)}) copy-start(f32[4,16,256,128]{3,2,1,0:T(8,128)S(1)} %get-tuple-element.357) | copy-start | bytes 25165828
  158.6 4.4 %copy-start.22 = (f32[4,2,8,128]{3,2,0,1:T(8,128)S(1)}, f32[4,2,8,128]{3,2,0,1:T(8,128)}, u32[]{:S(2)}) copy-start(f32[4,2,8,128]{3,2,0,1:T(8,128)} %copy.331) | copy-start | bytes 98308
  163.1 6.9 %copy-start.8 = (bf16[1,512,16,128]{3,2,1,0:T(8,128)(2,1)S(1)}, bf16[1,512,16,128]{3,2,1,0:T(8,128)(2,1)}, u32[]{:S(2)}) copy-start(bf16[1,512,16,128]{3,2,1,0:T(8,128)(2,1)} %param.17) | copy-start | bytes 6291460
  170.0 14.2 %copy-start.24 = (f32[4,16,1,128]{3,2,1,0:T(1,128)S(1)}, f32[4,16,1,128]{3,2,1,0:T(1,128)}, u32[]{:S(2)}) copy-start(f32[4,16,1,128]{3,2,1,0:T(1,128)} %copy-done.23) | copy-start | bytes 98308
  170.0 15.0 %copy-start.35 = (s32[4]{0:T(128)S(1)}, s32[4]{0:T(128)}, u32[]{:S(2)}) copy-start(s32[4]{0:T(128)} %copy-done.34) | copy-start | bytes 52
  170.0 16.6 %copy-start.28 = (f32[4,128,16]{1,2,0:T(8,128)S(1)}, f32[4,128,16]{1,2,0:T(8,128)}, u32[]{:S(2)}) copy-start(f32[4,128,16]{1,2,0:T(8,128)} %get-tuple-element.352) | copy-start | bytes 98308
  184.3 9.9 %copy-start.30 = (f32[4,128,16]{1,2,0:T(8,128)}, f32[4,128,16]{1,2,0:T(8,128)S(1)}, u32[]{:S(2)}) copy-start(f32[4,128,16]{1,2,0:T(8,128)S(1)} %get-tuple-element.350) | copy-start | bytes 98308
  184.3 9.9 %copy-start.31 = (f32[4,128,16]{1,2,0:T(8,128)}, f32[4,128,16]{1,2,0:T(8,128)S(1)}, u32[]{:S(2)}) copy-start(f32[4,128,16]{1,2,0:T(8,128)S(1)} %get-tuple-element.351) | copy-start | bytes 98308
  186.6 69.3 %copy-start.25 = (f32[16,8]{0,1:T(8,128)S(1)}, f32[16,8]{0,1:T(8,128)}, u32[]{:S(2)}) copy-start(f32[16,8]{0,1:T(8,128)} %custom-call.3) | copy-start | bytes 1540
  186.6 70.1 %copy-start.36 = (s32[4]{0:T(128)S(1)}, s32[4]{0:T(128)}, u32[]{:S(2)}) copy-start(s32[4]{0:T(128)} %copy-done.34) | copy-start | bytes 52
  186.6 70.1 %copy-start.39 = (f32[5]{0:T(128)S(1)}, f32[5]{0:T(128)}, u32[]{:S(2)}) copy-start(f32[5]{0:T(128)} %broadcast_subtract_fusion) | copy-start | bytes 64
  186.6 70.1 %copy-start.41 = (f32[5]{0:T(128)S(1)}, f32[5]{0:T(128)}, u32[]{:S(2)}) copy-start(f32[5]{0:T(128)} %compare_convert_fusion.1) | copy-start | bytes 64
  186.6 70.1 %copy-start.43 = (f32[5]{0:T(128)S(1)}, f32[5]{0:T(128)}, u32[]{:S(2)}) copy-start(f32[5]{0:T(128)} %compare_convert_fusion) | copy-start | bytes 64
  277.8 4.2 copy-start.6
  277.8 4.2 copy-start.18
  277.8 4.2 copy-start.20
  277.9 4.2 %copy-start.33 = (f32[640]{0:T(1024)S(1)}, f32[640]{0:T(1024)}, u32[]{:S(2)}) copy-start(f32[640]{0:T(1024)} %copy-done.32) | copy-start | bytes 7684
  (16 other events, 37.0 us)
Sparse Core Ops, SparseCore 0:
  285.3 124.7 all-reduce.3
where the time goes:
time: 427 us; the launch traced here: 420 us
  blocking collectives  128 us (30%)
  waiting for transfers between devices  118 us (28%)
  matrix products  64.9 us (15%)
  other arithmetic  52 us (12%)
  local copies, waits for them, and re-layouts  33.3 us (8%)
  between operations  15.1 us (4%)
  starting transfers between devices  8.39 us (2%)
    all_gather x4, blocking collectives, prefix(): everything = jax.tree.map(lambda part: lax.all_gather(part, axis), shard)  128 us
    psum x1, waiting for transfers between devices, body(): grad_q, grad_k = lax.psum((grad_q, grad_k), ('seq', 'batch'))  118 us
    reduce_sum x1, other arithmetic, body(): ratio_grad = -jnp.sum(delta * out, -1)  14.1 us
    unnamed x93, local copies, waits for them, and re-layouts  11.3 us
    dot_general x1, matrix products, body(): jnp.einsum('nthd,nhrd->nthr', grad_num, state, precision=HIGHEST)  9.54 us
  transfers between devices with their start and end apart: 3, of which 1 were waited for; matrix products, arithmetic and copies ran while one was open for 6% of the time, Pallas kernels for 0%

commit v1 on v0

--- a/solution.py
+++ b/solution.py
@@ -199,7 +199,7 @@
     grad_pre_q = grad_fq.reshape(tokens, heads, rank) * jax.nn.sigmoid(pre_q)
     grad_q = jnp.einsum("thd,thr->hdr", q_rows.astype(jnp.float32), grad_pre_q, precision=HIGHEST)
     grad_k = jnp.einsum("thd,thr->hdr", ext_keys.astype(jnp.float32), grad_pre_k, precision=HIGHEST)
-    grad_q, grad_k = lax.psum((grad_q, grad_k), ("seq", "batch"))
+    grad_q, grad_k = lax.psum(lax.psum((grad_q, grad_k), "seq"), "batch")
     return (out.astype(jnp.bfloat16)[None], grad_q, grad_k)
 
 

time: 427 us -> 406 us (0.951)
  waiting for transfers between devices: 118 us -> 96.8 us
    psum x1 -> x2, waiting for transfers between devices: 118 us -> 96.8 us  [body(): grad_q, grad_k = lax.psum(lax.psum((grad_q, grad_k), 'seq'), 'batch')]
  transfers between devices with their start and end apart: 3 -> 4, of which waited for: 1 -> 2; matrix products, arithmetic and copies ran while one was open for 6% -> 6% of each run, Pallas kernels for 0% -> 0%
where the time goes in v1:
time: 406 us; the launch traced here: 399 us
  blocking collectives  128 us (32%)
  waiting for transfers between devices  96.8 us (24%)
  matrix products  64.9 us (16%)
  other arithmetic  51.9 us (13%)
  local copies, waits for them, and re-layouts  33.3 us (8%)
  between operations  15.1 us (4%)
  starting transfers between devices  8.43 us (2%)
    all_gather x4, blocking collectives, prefix(): everything = jax.tree.map(lambda part: lax.all_gather(part, axis), shard)  128 us
    psum x2, waiting for transfers between devices, body(): grad_q, grad_k = lax.psum(lax.psum((grad_q, grad_k), 'seq'), 'batch')  96.8 us
    reduce_sum x1, other arithmetic, body(): ratio_grad = -jnp.sum(delta * out, -1)  14.1 us
    unnamed x93, local copies, waits for them, and re-layouts  11.3 us
    dot_general x1, matrix products, body(): jnp.einsum('nthd,nhrd->nthr', grad_num, state, precision=HIGHEST)  9.54 us
    ppermute x2, starting transfers between devices, passed_along(): lax.ppermute(value, axis, [(source, source + steps) for source in range(f...  8.35 us
  transfers between devices with their start and end apart: 4, of which 2 were waited for; matrix products, arithmetic and copies ran while one was open for 6% of the time, Pallas kernels for 0%

profile of v1, /device:TPU:0, one launch (start us, length us, event | category | flops | bytes accessed | tf_op | source)
XLA Modules:
  0.0 399.4 jit_solution(13520086422673321246)
XLA Ops:
  7.2 2.3 copy.332
  11.7 5.7 %collective-permute-start.1 = (bf16[128,16,128]{2,0,1:T(8,128)(2,1)}, bf16[128,16,128]{2,0,1:T(8,128)(2,1)}, u32[]{:S(2)}, u32[]{:S(2)}) collective-permute-start(bf16[128,16,128]{2,0,1:T(8,128)(2,1)} %slice_bitcast_fusion), channel_id=1, source_target_pairs={{0,4},{4,8},{8,12},{12,16},{16,20},{20,24},{24,28},{1,5},{5,9},{9,... | collective-permute-start | bytes 1572872 | tf_op jit(solution)/shard_map/ppermute | solution.py:16
  19.3 2.7 collective-permute-start
  25.8 3.5 copy.177
  29.3 1.9 copy.171
  31.3 2.4 convert.3
  35.2 2.0 fusion.65
  43.0 2.1 fusion.44
  45.1 35.4 %all-gather = f32[128,8,128]{2,1,0:T(8,128)} all-gather(f32[16,8,128]{2,1,0:T(8,128)S(1)} %slice_reduce_fusion), channel_id=2, replica_groups=mesh['seq'=8,'batch'=4] {'seq'}, dimensions={0}, use_global_device_ids=true | all-gather | bytes 589824 | tf_op jit(solution)/shard_map/all_gather | solution.py:21
  80.6 30.6 %all-gather.4 = f32[8,16,8]{1,2,0:T(8,128)S(1)} all-gather(f32[1,16,8]{1,2,0:T(8,128)S(1)} %bitcast.246), channel_id=3, replica_groups=mesh['seq'=8,'batch'=4] {'seq'}, dimensions={0}, use_global_device_ids=true | all-gather | bytes 4608 | tf_op jit(solution)/shard_map/all_gather | solution.py:21
  111.2 7.7 %while.34 = (s32[]{:T(128)}, f32[16,8,128]{2,1,0:T(8,128)S(1)}, f32[16,8]{0,1:T(8,128)S(1)}, s32[]{:T(128)}, f32[8,16,8,128]{3,2,1,0:T(8,128)}, /*index=5*/f32[8,16,8]{1,2,0:T(8,128)S(1)}, s32[]{:T(128)}, s32[]{:T(128)}) while((s32[]{:T(128)}, f32[16,8,128]{2,1,0:T(8,128)S(1)}, f32[16,8]{0,1:T(8,128)S(1)}, s32[]{:T(128)}, ...), condition=%wide.region_5.6_spmd.clone, body=%wide.region_4.5_spmd.clone.sunk | while | flops 49540 | bytes 198259 | solution.py:34
  118.9 3.9 fusion.42
  124.9 6.7 %convolution_bitcast_fusion = f32[4,128,16,128]{3,1,2,0:T(8,128)S(1)} fusion(f32[4,16,8,128]{3,0,2,1:T(4,128)S(1)} %fusion.66, f32[512,16,8]{0,2,1:T(8,128)S(1)} %copy-done.13), kind=kOutput, calls=%fused_computation.42 | convolution fusion | flops 101056512 | bytes 4718592 | tf_op jit(solution)/shard_map/nthr,nhrd->nthd/dot_general | solution.py:155
  131.6 4.5 %copy.193 = f32[4,128,16,128]{3,2,1,0:T(8,128)} copy(f32[4,128,16,128]{3,1,2,0:T(8,128)S(1)} %convolution_bitcast_fusion) | data formatting | bytes 8388608 | tf_op jit(solution)/shard_map/nthr,nhrd->nthd/transpose | solution.py:155
  139.9 2.9 fusion
  143.5 4.1 %fusion.2 = f32[4,16,128]{2,1,0:T(8,128)S(1)} fusion(f32[4,16,256,128]{3,2,1,0:T(8,128)S(1)} %get-tuple-element.359, f32[4,16,128]{2,1,0:T(8,128)S(1)} %get-tuple-element.358, pred[4,16,256]{2,1,0:T(8,128)(4,1)S(1)} %copy-done.26, pred[128,256]{0,1:T(8,128)(4,1)S(1)} %copy-done.21, pred[256]{0:T(512)(128)(4,1)S(1)} %copy-done.42), kind=kLoop, calls=%fused_computation.9 | loop fusion | flops 10477568 | bytes 8503552 | tf_op jit(solution)/shard_map/reduce_sum | solution.py:146
  152.3 6.3 %fusion.27 = f32[4,128,16,128]{3,1,2,0:T(8,128)S(1)} fusion(f32[4,16,256,128]{3,2,1,0:T(8,128)S(1)} %copy-done.10, f32[4,16,128]{2,1,0:T(8,128)S(1)} %get-tuple-element.358, pred[4,16,256]{2,1,0:T(8,128)(4,1)S(1)} %copy-done.26, pred[128,256]{0,1:T(8,128)(4,1)S(1)} %copy-done.21, pred[256]{0:T(512)(128)(4,1)S(1)} %copy-done.42, ...), kind=kOutput, calls=%fused_computation.41 | convolution fusion | flops 555745280 | bytes 16859392 | tf_op jit(solution)/shard_map/nhqk,nkhd->nqhd/dot_general | solution.py:147
  158.6 4.4 %copy.180 = f32[4,128,16,128]{3,2,1,0:T(8,128)} copy(f32[4,128,16,128]{3,1,2,0:T(8,128)S(1)} %fusion.27) | data formatting | bytes 8388608 | tf_op jit(solution)/shard_map/nhqk,nkhd->nqhd/transpose | solution.py:147
  163.1 6.9 %fusion.14 = f32[512,16,128]{2,1,0:T(8,128)S(1)} fusion(f32[4,128,16,128]{3,2,1,0:T(8,128)} %copy.193, f32[4,128,16,128]{3,2,1,0:T(8,128)} %copy.180, f32[512,16]{1,0:T(8,128)S(1)} %copy.182, f32[512,16]{1,0:T(8,128)S(1)} %copy.198), kind=kLoop, calls=%fused_computation.21 | loop fusion | flops 3145728 | bytes 12648448 | tf_op jit(solution)/shard_map/div | solution.py:162
  170.0 14.1 %fusion.23 = f32[512,16]{1,0:T(8,128)S(1)} fusion(f32[512,16,128]{2,1,0:T(8,128)S(1)} %fusion.14, f32[512,16]{1,0:T(8,128)S(1)} %copy.198, bf16[1,512,16,128]{3,2,1,0:T(8,128)(2,1)S(1)} %copy-done.8), kind=kLoop, calls=%fused_computation.33 | loop fusion | flops 4186112 | bytes 6356992 | tf_op jit(solution)/shard_map/reduce_sum | solution.py:164
  186.7 7.5 %fusion.174 = (f32[16,8,128]{2,1,0:T(8,128)S(1)}, f32[4,16,8,128]{3,2,1,0:T(8,128)}) fusion(f32[4,128,16,128]{3,2,1,0:T(8,128)} %convert.3, f32[4,128,16]{1,2,0:T(8,128)S(1)} %get-tuple-element.353, f32[4,128,16]{1,2,0:T(8,128)S(1)} %copy-done.28, f32[512,16,8]{0,2,1:T(8,128)S(1)} %copy-done.14), kind=kOutput, calls=%fused_computation.200 | convolution fusion | flops 103202816 | bytes 4849664 | tf_op jit(solution)/shard_map/nthr,nthd->nhrd/dot_general | solution.py:171
  194.2 31.2 %all-gather.2 = f32[128,8,128]{2,1,0:T(8,128)S(1)} all-gather(f32[16,8,128]{2,1,0:T(8,128)S(1)} %get-tuple-element.360), channel_id=4, replica_groups=mesh['seq'=8,'batch'=4] {'seq'}, dimensions={0}, use_global_device_ids=true | all-gather | bytes 589824 | tf_op jit(solution)/shard_map/all_gather | solution.py:21
  225.4 30.6 %all-gather.5 = f32[8,16,8]{1,2,0:T(8,128)S(1)} all-gather(f32[1,16,8]{1,2,0:T(8,128)S(1)} %bitcast.245), channel_id=5, replica_groups=mesh['seq'=8,'batch'=4] {'seq'}, dimensions={0}, use_global_device_ids=true | all-gather | bytes 4608 | tf_op jit(solution)/shard_map/all_gather | solution.py:21
  258.7 2.6 convolution_add_fusion
  262.2 9.5 %fusion.76 = f32[4,128,16,8]{1,3,2,0:T(8,128)S(1)} fusion(f32[4,128,16,128]{3,2,1,0:T(8,128)} %convert.3, f32[4,128,16]{1,2,0:T(8,128)} %copy-done.31, f32[4,128,16]{1,2,0:T(8,128)} %get-tuple-element.354, f32[4,16,8,128]{3,0,2,1:T(4,128)} %copy-done.15, f32[4,16,8]{2,1,0:T(8,128)} %copy.207, f32[4,128,16]{1,2,0:T(8,128)} %copy-done.30), kind=kOutput, calls=%fused_computation.74 | convolution fusion | flops 102891520 | bytes 4818944 | tf_op jit(solution)/shard_map/nthd,nhrd->nthr/dot_general | solution.py:168
  271.7 2.0 fusion.79
  273.7 4.1 %fusion.51 = f32[5,128,16,8]{1,3,2,0:T(8,128)S(1)} fusion(bf16[5,128,16,128]{3,2,1,0:T(8,128)(2,1)S(1)} %bitcast.225, f32[5,16,8,128]{3,0,2,1:T(8,128)S(1)} %copy-done.16, f32[5,16,8]{2,1,0:T(8,128)S(1)} %copy.214), kind=kOutput, calls=%fused_computation.62 | convolution fusion | flops 125911040 | bytes 3279360 | tf_op jit(solution)/shard_map/nhrd,nthd->nthr/dot_general | solution.py:193
  277.9 4.1 %fusion.57 = f32[5,128,16,8]{1,3,2,0:T(8,128)S(1)} fusion(bf16[5,128,16,128]{3,2,1,0:T(8,128)(2,1)S(1)} %bitcast.226, f32[5,16,8,128]{3,0,2,1:T(8,128)S(1)} %fusion.106, f32[5,16,8]{2,1,0:T(8,128)S(1)} %copy.219), kind=kOutput, calls=%fused_computation.64 | convolution fusion | flops 125911040 | bytes 3279360 | tf_op jit(solution)/shard_map/nhrd,nthd->nthr/dot_general | solution.py:194
  282.1 3.1 fusion.47
  285.2 70.7 %all-reduce.6.cloned.1.call-done = (f32[16,128,8]{1,2,0:T(8,128)}, f32[16,128,8]{1,2,0:T(8,128)}) async-done(((f32[16,128,8]{1,2,0:T(8,128)}, f32[16,128,8]{1,2,0:T(8,128)}), (f32[16,128,8]{1,2,0:T(8,128)}, f32[16,128,8]{1,2,0:T(8,128)})) %all-reduce.6.cloned.1.call-update) | async-done | bytes 131088 | tf_op jit(solution)/shard_map/psum | solution.py:202
  355.9 7.2 %fusion.18 = bf16[1,512,16,128]{3,2,1,0:T(8,128)(2,1)} fusion(f32[512,16]{1,0:T(8,128)S(1)} %copy.198, f32[512,16]{1,0:T(8,128)S(1)} %copy.182, f32[1,512,16,128]{3,2,1,0:T(8,128)} %bitcast.221, f32[1,512,16,128]{3,2,1,0:T(8,128)} %bitcast.222), kind=kLoop, calls=%fused_computation.27 | loop fusion | flops 4194304 | bytes 10551296 | tf_op jit(solution)/shard_map/convert_element_type | solution.py:203
  363.2 26.1 %all-reduce.8.cloned.1.call-done = (f32[16,128,8]{1,2,0:T(8,128)}, f32[16,128,8]{1,2,0:T(8,128)}) async-done(((f32[16,128,8]{1,2,0:T(8,128)}, f32[16,128,8]{1,2,0:T(8,128)}), (f32[16,128,8]{1,2,0:T(8,128)}, f32[16,128,8]{1,2,0:T(8,128)})) %all-reduce.8.cloned.1.call-update) | async-done | bytes 131088 | tf_op jit(solution)/shard_map/psum | solution.py:202
  (189 shorter events, 42.7 us)
Async XLA Ops:
  7.2 26.5 %copy-start = (bf16[1,512,16,128]{3,2,1,0:T(8,128)(2,1)S(1)}, bf16[1,512,16,128]{3,2,1,0:T(8,128)(2,1)}, u32[]{:S(2)}) copy-start(bf16[1,512,16,128]{3,2,1,0:T(8,128)(2,1)} %param.11) | copy-start | bytes 6291460
  7.2 16.6 %copy-start.37 = (s32[1,16,32]{2,1,0:T(8,128)S(1)}, s32[1,16,32]{2,1,0:T(8,128)}, u32[]{:S(2)}) copy-start(s32[1,16,32]{2,1,0:T(8,128)} %param.14) | copy-start | bytes 6148
  7.2 348.7 %all-reduce.6.cloned.1.call-start = ((), (), s32[]{:S(2)}) async-start(), calls=%async_computation | async-start | bytes 262144 | tf_op jit(solution)/shard_map/psum | solution.py:202
  11.7 23.5 %collective-permute-start.1 = (bf16[128,16,128]{2,0,1:T(8,128)(2,1)}, bf16[128,16,128]{2,0,1:T(8,128)(2,1)}, u32[]{:S(2)}, u32[]{:S(2)}) collective-permute-start(bf16[128,16,128]{2,0,1:T(8,128)(2,1)} %slice_bitcast_fusion), channel_id=1, source_target_pairs={{0,4},{4,8},{8,12},{12,16},{16,20},{20,24},{24,28},{1,5},{5,9},{9,... | collective-permute-start | bytes 1572872 | tf_op jit(solution)/shard_map/ppermute | solution.py:16
  19.3 20.3 %collective-permute-start = (bf16[128,16,128]{2,1,0:T(8,128)(2,1)}, bf16[128,16,128]{2,1,0:T(8,128)(2,1)S(1)}, u32[]{:S(2)}, u32[]{:S(2)}) collective-permute-start(bf16[128,16,128]{2,1,0:T(8,128)(2,1)} %slice_bitcast_fusion.1), channel_id=1, source_target_pairs={{0,4},{4,8},{8,12},{12,16},{16,20},{20,24},{24,28},{1,5},{5,9},{9,... | collective-permute-start | bytes 1572872 | tf_op jit(solution)/shard_map/ppermute | solution.py:16
  22.0 15.2 %copy-start.32 = (f32[640]{0:T(1024)}, f32[640]{0:T(1024)S(1)}, u32[]{:S(2)}) copy-start(f32[640]{0:T(1024)S(1)} %fusion.149) | copy-start | bytes 7684
  22.0 114.2 %copy-start.34 = (s32[4]{0:T(128)}, s32[4]{0:T(128)S(1)}, u32[]{:S(2)}) copy-start(s32[4]{0:T(128)S(1)} %iota_add_fusion.1) | copy-start | bytes 52
  25.2 4.1 %copy-start.3 = (bf16[1,512,16,128]{3,2,1,0:T(8,128)(2,1)S(1)}, bf16[1,512,16,128]{3,2,1,0:T(8,128)(2,1)}, u32[]{:S(2)}) copy-start(bf16[1,512,16,128]{3,2,1,0:T(8,128)(2,1)} %param.13) | copy-start | bytes 6291460
  111.2 12.2 %copy-start.38 = (f32[5]{0:T(128)S(1)}, f32[5]{0:T(128)}, u32[]{:S(2)}) copy-start(f32[5]{0:T(128)} %broadcast_subtract_fusion) | copy-start | bytes 64
  111.2 12.2 %copy-start.40 = (f32[5]{0:T(128)S(1)}, f32[5]{0:T(128)}, u32[]{:S(2)}) copy-start(f32[5]{0:T(128)} %compare_convert_fusion.1) | copy-start | bytes 64
  118.8 6.0 %copy-start.13 = (f32[512,16,8]{0,2,1:T(8,128)S(1)}, f32[512,16,8]{0,2,1:T(8,128)}, u32[]{:S(2)}) copy-start(f32[512,16,8]{0,2,1:T(8,128)} %fusion.73) | copy-start | bytes 786436
  131.6 4.7 %copy-start.29 = (f32[5,16,8]{1,0,2:T(8,128)S(1)}, f32[5,16,8]{1,0,2:T(8,128)}, u32[]{:S(2)}) copy-start(f32[5,16,8]{1,0,2:T(8,128)} %copy.195) | copy-start | bytes 7684
  131.6 5.9 %copy-start.14 = (f32[512,16,8]{0,2,1:T(8,128)S(1)}, f32[512,16,8]{0,2,1:T(8,128)}, u32[]{:S(2)}) copy-start(f32[512,16,8]{0,2,1:T(8,128)} %fusion.73) | copy-start | bytes 786436
  138.2 10.1 %copy-start.23 = (f32[4,16,1,128]{3,2,1,0:T(1,128)}, f32[4,16,1,128]{3,2,1,0:T(1,128)S(1)}, u32[]{:S(2)}) copy-start(f32[4,16,1,128]{3,2,1,0:T(1,128)S(1)} %fusion.112) | copy-start | bytes 98308
  142.8 4.8 %copy-start.9 = (f32[4,16,256,128]{3,2,1,0:T(8,128)}, f32[4,16,256,128]{3,2,1,0:T(8,128)S(1)}, u32[]{:S(2)}) copy-start(f32[4,16,256,128]{3,2,1,0:T(8,128)S(1)} %get-tuple-element.359) | copy-start | bytes 25165828
  158.6 4.4 %copy-start.22 = (f32[4,2,8,128]{3,2,0,1:T(8,128)S(1)}, f32[4,2,8,128]{3,2,0,1:T(8,128)}, u32[]{:S(2)}) copy-start(f32[4,2,8,128]{3,2,0,1:T(8,128)} %copy.331) | copy-start | bytes 98308
  163.1 6.9 %copy-start.8 = (bf16[1,512,16,128]{3,2,1,0:T(8,128)(2,1)S(1)}, bf16[1,512,16,128]{3,2,1,0:T(8,128)(2,1)}, u32[]{:S(2)}) copy-start(bf16[1,512,16,128]{3,2,1,0:T(8,128)(2,1)} %param.17) | copy-start | bytes 6291460
  170.0 14.2 %copy-start.24 = (f32[4,16,1,128]{3,2,1,0:T(1,128)S(1)}, f32[4,16,1,128]{3,2,1,0:T(1,128)}, u32[]{:S(2)}) copy-start(f32[4,16,1,128]{3,2,1,0:T(1,128)} %copy-done.23) | copy-start | bytes 98308
  170.0 15.0 %copy-start.35 = (s32[4]{0:T(128)S(1)}, s32[4]{0:T(128)}, u32[]{:S(2)}) copy-start(s32[4]{0:T(128)} %copy-done.34) | copy-start | bytes 52
  170.0 16.6 %copy-start.28 = (f32[4,128,16]{1,2,0:T(8,128)S(1)}, f32[4,128,16]{1,2,0:T(8,128)}, u32[]{:S(2)}) copy-start(f32[4,128,16]{1,2,0:T(8,128)} %get-tuple-element.354) | copy-start | bytes 98308
  184.2 9.9 %copy-start.30 = (f32[4,128,16]{1,2,0:T(8,128)}, f32[4,128,16]{1,2,0:T(8,128)S(1)}, u32[]{:S(2)}) copy-start(f32[4,128,16]{1,2,0:T(8,128)S(1)} %get-tuple-element.352) | copy-start | bytes 98308
  184.3 9.9 %copy-start.31 = (f32[4,128,16]{1,2,0:T(8,128)}, f32[4,128,16]{1,2,0:T(8,128)S(1)}, u32[]{:S(2)}) copy-start(f32[4,128,16]{1,2,0:T(8,128)S(1)} %get-tuple-element.353) | copy-start | bytes 98308
  186.6 69.3 %copy-start.25 = (f32[16,8]{0,1:T(8,128)S(1)}, f32[16,8]{0,1:T(8,128)}, u32[]{:S(2)}) copy-start(f32[16,8]{0,1:T(8,128)} %custom-call.3) | copy-start | bytes 1540
  186.6 70.1 %copy-start.36 = (s32[4]{0:T(128)S(1)}, s32[4]{0:T(128)}, u32[]{:S(2)}) copy-start(s32[4]{0:T(128)} %copy-done.34) | copy-start | bytes 52
  186.6 70.1 %copy-start.39 = (f32[5]{0:T(128)S(1)}, f32[5]{0:T(128)}, u32[]{:S(2)}) copy-start(f32[5]{0:T(128)} %broadcast_subtract_fusion) | copy-start | bytes 64
  186.6 70.1 %copy-start.41 = (f32[5]{0:T(128)S(1)}, f32[5]{0:T(128)}, u32[]{:S(2)}) copy-start(f32[5]{0:T(128)} %compare_convert_fusion.1) | copy-start | bytes 64
  186.6 70.1 %copy-start.43 = (f32[5]{0:T(128)S(1)}, f32[5]{0:T(128)}, u32[]{:S(2)}) copy-start(f32[5]{0:T(128)} %compare_convert_fusion) | copy-start | bytes 64
  277.9 4.2 %copy-start.6 = (bf16[1,512,16,128]{3,1,2,0:T(8,128)(2,1)S(1)}, bf16[1,512,16,128]{3,1,2,0:T(8,128)(2,1)}, u32[]{:S(2)}) copy-start(bf16[1,512,16,128]{3,1,2,0:T(8,128)(2,1)} %copy-done.4) | copy-start | bytes 6291460
  277.9 4.2 %copy-start.18 = (f32[640,16,8]{0,2,1:T(8,128)S(1)}, f32[640,16,8]{0,2,1:T(8,128)}, u32[]{:S(2)}) copy-start(f32[640,16,8]{0,2,1:T(8,128)} %copy-done.17) | copy-start | bytes 983044
  277.9 4.2 %copy-start.20 = (f32[640,16]{0,1:T(8,128)S(1)}, f32[640,16]{0,1:T(8,128)}, u32[]{:S(2)}) copy-start(f32[640,16]{0,1:T(8,128)} %copy-done.19) | copy-start | bytes 122884
  277.9 4.2 %copy-start.33 = (f32[640]{0:T(1024)S(1)}, f32[640]{0:T(1024)}, u32[]{:S(2)}) copy-start(f32[640]{0:T(1024)} %copy-done.32) | copy-start | bytes 7684
  285.2 104.1 %all-reduce.8.cloned.1.call-start = ((), (), s32[]{:S(2)}) async-start(), calls=%async_computation.1 | async-start | bytes 262144 | tf_op jit(solution)/shard_map/psum | solution.py:202
  (17 other events, 40.9 us)
Sparse Core Ops, SparseCore 0:
  285.3 70.5 all-reduce.5
  358.3 30.9 all-reduce.7
